TPU v7x, 512 devices: a whole 4x8x8 slice. The times are simulated.
512 devices in a mesh: rows: 512 (over z, y, x, core).
Axes of the slice: x: 4, y: 8, z: 8, core: 2. Of those that a mesh axis runs over, the one named last changes fastest.
Arguments:
- adj_diag: int32 [8192, 512], P('rows'), may hold values from -2147483648 to 2147483647
- adj_right: int32 [8192, 512], P('rows'), may hold values from -2147483648 to 2147483647
- alive_diag: int32 [8192, 512], P('rows'), may hold values from -2147483648 to 2147483647
- alive_right: int32 [8192, 512], P('rows'), may hold values from -2147483648 to 2147483647
- truss_k: int32 [1], replicated, may hold values from 130 to 193
Outputs:
- support_field: float32 [262144, 1024], P('rows')
- removed_counts: int32 [3], replicated
All inputs are finite; a program needn't handle non-finite values.
Results may differ from a plain program's by a relative error of at most 0.0003.
Values may be sent and summed in bfloat16 or wider, within the bound.
A program may use at most 64 MiB of HBM per device.

v0:
```python
import jax
import jax.numpy as jnp
from jax import lax
from jax.sharding import Mesh
from jax.sharding import PartitionSpec as P

ITERS = 3
ROWS = ("rows_0", "rows_1", "rows_2", "rows_3")


def shifted(array, axis, by):
    count = lax.axis_size(axis)
    return lax.ppermute(array, axis, [(i, (i + by) % count) for i in range(count)])


def over_axes(array, axes):
    for axis in axes:
        array = lax.psum(array, axis)
    return array


def unpack_tile(packed):
    shifts = jnp.arange(32, dtype=jnp.int32)
    tile_bits = packed[:, None, :] >> shifts[None, :, None] & 1
    return tile_bits.reshape(packed.shape[0] * 32, packed.shape[1])


def pack_bits(tile_bits):
    shifts = jnp.arange(32, dtype=jnp.int32)
    sectioned = tile_bits.reshape(tile_bits.shape[0] // 32, 32, tile_bits.shape[1])
    return jnp.sum(sectioned << shifts[None, :, None], axis=1, dtype=jnp.int32)


def within_tile(packed):
    upper_half = jnp.triu(unpack_tile(packed), 1)
    return (upper_half + upper_half.T).astype(jnp.bfloat16)


def across_tile(packed):
    return unpack_tile(packed).astype(jnp.bfloat16)


def pack_across(across):
    return pack_bits(across.astype(jnp.int32))


def fold_within(within):
    width = within.shape[0]
    half = width // 2
    row_ids = lax.broadcasted_iota(jnp.int32, (half, width), 0)
    col_ids = lax.broadcasted_iota(jnp.int32, (half, width), 1)
    flipped = within[half:][::-1, ::-1]
    folded = jnp.where(col_ids > row_ids, within[:half], flipped)
    return pack_bits(folded.astype(jnp.int32))


def unfold_within(packed):
    folded = unpack_tile(packed)
    half = folded.shape[0]
    width = folded.shape[1]
    row_ids = lax.broadcasted_iota(jnp.int32, (half, width), 0)
    col_ids = lax.broadcasted_iota(jnp.int32, (half, width), 1)
    top_rows = jnp.where(col_ids > row_ids, folded, jnp.zeros_like(folded))
    bottom_rows = jnp.where(col_ids < row_ids, folded, jnp.zeros_like(folded))[::-1, ::-1]
    upper_half = jnp.concatenate([top_rows, bottom_rows], axis=0)
    return (upper_half + upper_half.T).astype(jnp.bfloat16)


def support_within(prev_across, within, across):
    inside = lax.dot_general(
        prev_across, prev_across, (((0,), (0,)), ((), ())), preferred_element_type=jnp.float32
    )
    inside = inside + jnp.dot(within, within, preferred_element_type=jnp.float32)
    return inside + lax.dot_general(
        across, across, (((1,), (1,)), ((), ())), preferred_element_type=jnp.float32
    )


def support_across(within, across, next_within):
    between = jnp.dot(within, across, preferred_element_type=jnp.float32)
    return between + jnp.dot(across, next_within, preferred_element_type=jnp.float32)


def keep_edges(support, tile_mask, thresh):
    return jnp.where(support >= thresh, tile_mask, jnp.zeros_like(tile_mask))


def peel(prev_across, within, across, next_within, thresh):
    inside = support_within(prev_across, within, across)
    between = support_across(within, across, next_within)
    return (
        inside,
        between,
        keep_edges(inside, within, thresh),
        keep_edges(between, across, thresh),
    )


def tally(within, new_within, across, new_across):
    removed = jnp.sum((within - new_within).astype(jnp.int32)) // 2
    removed = removed + jnp.sum((across - new_across).astype(jnp.int32))
    return removed


def on_device(adj_diag, adj_right, alive_diag, alive_right, truss_k):
    within = within_tile(adj_diag & alive_diag)
    across_words = adj_right & alive_right
    across = across_tile(across_words)
    thresh = (truss_k[0] - 2).astype(jnp.float32)
    counts = []
    for step in range(ITERS):
        prev_across = across_tile(shifted(pack_across(across), ROWS, 1))
        next_within = unfold_within(shifted(fold_within(within), ROWS, -1))
        inside, between, new_within, new_across = peel(
            prev_across, within, across, next_within, thresh
        )
        counts.append(tally(within, new_within, across, new_across))
        within, across = (new_within, new_across)
    stacked = jnp.stack(counts)
    stacked = over_axes(stacked, ROWS)
    support = jnp.concatenate(
        [inside * within.astype(jnp.float32), between * across.astype(jnp.float32)], axis=1
    )
    return (support, stacked)


def solution(mesh):
    split = Mesh(mesh.devices.reshape(8, 8, 4, 2), ("rows_0", "rows_1", "rows_2", "rows_3"))
    placed = (P(ROWS, None), P(ROWS, None), P(ROWS, None), P(ROWS, None), P())
    return jax.shard_map(
        on_device, mesh=split, in_specs=placed, out_specs=(P(ROWS, None), P()), check_vma=False
    )
```

profile of v0, /device:TPU:1, one launch (start us, length us, event | category | flops | bytes accessed | tf_op | source)
XLA Modules:
  0.0 128.3 jit_solution(3447967203919431901)
XLA Ops:
  0.6 0.0 copy-start.4
  0.6 0.0 copy-start.5
  0.7 0.1 shift_right_arithmetic.162
  0.7 0.8 and.74
  1.5 0.2 fusion.17
  1.7 0.3 copy.7
  2.1 0.3 fusion.14
  2.4 0.9 rev.18
  3.4 0.1 fusion.25
  3.5 8.7 %collective-permute-start.1 = (s32[8,512]{1,0:T(8,128)S(1)}, s32[8,512]{1,0:T(8,128)S(1)}, u32[]{:S(2)}, u32[]{:S(2)}) collective-permute-start(s32[8,512]{1,0:T(8,128)S(1)} %fusion.25), channel_id=1, source_target_pairs={{0,511},{1,0},{2,1},{3,2},{4,3},{5,4},{6,5},{7,6},{8,7},{9,8},{10,... | collective-permute-start | bytes 49160 | tf_op jit(solution)/shard_map/ppermute | solution.py:13
  12.2 0.4 and_convert_fusion.3
  12.6 1.9 %collective-permute-start = (s32[16,512]{1,0:T(8,128)S(1)}, s32[16,512]{1,0:T(8,128)S(1)}, u32[]{:S(2)}, u32[]{:S(2)}) collective-permute-start(s32[16,512]{1,0:T(8,128)S(1)} %get-tuple-element.9), channel_id=1, source_target_pairs={{0,1},{1,2},{2,3},{3,4},{4,5},{5,6},{6,7},{7,8},{8,9},{9,10},{10,1... | collective-permute-start | bytes 98312 | tf_op jit(solution)/shard_map/ppermute | solution.py:13
  14.6 1.4 %fusion.47 = f32[512,512]{1,0:T(8,128)} fusion(bf16[512,512]{1,0:T(8,128)(2,1)S(1)} %get-tuple-element.17, bf16[512,512]{1,0:T(8,128)(2,1)S(1)} %get-tuple-element.16), kind=kOutput, calls=%fused_computation.93 | convolution fusion | flops 268435456 | bytes 2097152 | tf_op jit(solution)/shard_map/dot_general | solution.py:80
  16.0 0.1 shift_left.64
  16.7 0.0 collective-permute-done.1
  16.7 0.1 fusion.34
  16.9 0.8 rev.19
  17.6 1.1 pad_add_fusion
  18.7 2.6 %copy.8 = s32[512,512]{0,1:T(8,128)} copy(s32[512,512]{1,0:T(8,128)} %pad_add_fusion) | data formatting | bytes 2097152 | tf_op jit(solution)/shard_map/concatenate | solution.py:65
  21.3 2.2 %fusion.8 = (s32[16,512]{1,0:T(8,128)S(1)}, bf16[512,512]{1,0:T(8,128)(2,1)S(1)}) fusion(bf16[512,512]{1,0:T(8,128)(2,1)S(1)} %get-tuple-element.16, f32[]{:T(128)} %bitcast.4, f32[512,512]{1,0:T(8,128)} %fusion.47, s32[512,512]{0,1:T(8,128)} %copy.8, s32[256,512]{1,0:T(8,128)S(1)} %rev.19, s32[256,512]{1,0:T(8,128)S(1)} %get-tuple-element.14), kind=kOutput, calls=%fused_computation.25 | convolution fusion | flops 270786560 | bytes 4227076 | tf_op jit(solution)/shard_map/dot_general | solution.py:81
  23.5 1.9 %collective-permute-start.4 = (s32[16,512]{1,0:T(8,128)S(1)}, s32[16,512]{1,0:T(8,128)S(1)}, u32[]{:S(2)}, u32[]{:S(2)}) collective-permute-start(s32[16,512]{1,0:T(8,128)S(1)} %get-tuple-element.20), channel_id=1, source_target_pairs={{0,1},{1,2},{2,3},{3,4},{4,5},{5,6},{6,7},{7,8},{8,9},{9,10},{10,1... | collective-permute-start | bytes 98312 | tf_op jit(solution)/shard_map/ppermute | solution.py:13
  25.5 0.0 collective-permute-done
  25.5 0.5 convolution_bitcast_fusion.2
  26.0 0.4 convolution_add_fusion.8
  26.4 0.5 fusion.7
  26.9 0.9 rev.20
  27.8 0.1 fusion.24
  28.0 10.1 %collective-permute-start.2 = (s32[8,512]{1,0:T(8,128)S(1)}, s32[8,512]{1,0:T(8,128)S(1)}, u32[]{:S(2)}, u32[]{:S(2)}) collective-permute-start(s32[8,512]{1,0:T(8,128)S(1)} %fusion.24), channel_id=1, source_target_pairs={{0,511},{1,0},{2,1},{3,2},{4,3},{5,4},{6,5},{7,6},{8,7},{9,8},{10,... | collective-permute-start | bytes 49160 | tf_op jit(solution)/shard_map/ppermute | solution.py:13
  38.1 0.0 collective-permute-done.4
  38.1 0.5 convolution_bitcast_fusion
  38.6 0.4 convolution_add_fusion.4
  39.1 0.5 fusion.6
  39.6 0.9 rev.22
  40.5 0.1 fusion.23
  40.6 9.1 %collective-permute-start.5 = (s32[8,512]{1,0:T(8,128)S(1)}, s32[8,512]{1,0:T(8,128)S(1)}, u32[]{:S(2)}, u32[]{:S(2)}) collective-permute-start(s32[8,512]{1,0:T(8,128)S(1)} %fusion.23), channel_id=1, source_target_pairs={{0,511},{1,0},{2,1},{3,2},{4,3},{5,4},{6,5},{7,6},{8,7},{9,8},{10,... | collective-permute-start | bytes 49160 | tf_op jit(solution)/shard_map/ppermute | solution.py:13
  49.7 1.4 %fusion.48 = f32[512,512]{1,0:T(8,128)} fusion(bf16[512,512]{1,0:T(8,128)(2,1)S(1)} %fusion.7, bf16[512,512]{1,0:T(8,128)(2,1)S(1)} %get-tuple-element.21), kind=kOutput, calls=%fused_computation.94 | convolution fusion | flops 268435456 | bytes 2097152 | tf_op jit(solution)/shard_map/dot_general | solution.py:80
  51.1 0.0 collective-permute-done.2
  51.1 0.0 collective-permute-done.5
  51.1 1.4 %fusion.28 = (s32[256,512]{1,0:T(8,128)}, s32[256,512]{1,0:T(8,128)}, s32[256,512]{1,0:T(8,128)}, s32[256,512]{1,0:T(8,128)S(1)}) fusion(s32[8,512]{1,0:T(8,128)S(1)} %collective-permute-done.5, s32[256]{0:T(256)S(1)} %shift_left.64, s32[8,512]{1,0:T(8,128)S(1)} %collective-permute-done.2), kind=kLoop, calls=%fused_computation.69 | loop fusion | flops 1310720 | bytes 2130944 | tf_op jit(solution)/shard_map/jit(_where)/select_n | solution.py:63
  52.5 3.9 %rev.21 = s32[256,512]{1,0:T(8,128)S(1)} reverse(s32[256,512]{1,0:T(8,128)} %get-tuple-element.18), dimensions={0,1} | reverse | bytes 1048576 | tf_op jit(solution)/shard_map/rev | solution.py:64
  56.4 1.1 pad_add_fusion.1
  57.5 0.0 copy-done.1
  57.5 2.6 %copy.9 = s32[512,512]{0,1:T(8,128)} copy(s32[512,512]{1,0:T(8,128)} %pad_add_fusion.1) | data formatting | bytes 2097152 | tf_op jit(solution)/shard_map/concatenate | solution.py:65
  60.1 2.4 %fusion.9 = (s32[16,512]{1,0:T(8,128)S(1)}, bf16[512,512]{1,0:T(8,128)(2,1)S(1)}) fusion(bf16[512,512]{1,0:T(8,128)(2,1)S(1)} %get-tuple-element.21, f32[]{:T(128)} %bitcast.4, f32[512,512]{1,0:T(8,128)} %fusion.48, s32[512,512]{0,1:T(8,128)} %copy.9, s32[256,512]{1,0:T(8,128)S(1)} %rev.21, s32[256,512]{1,0:T(8,128)} %copy-done.1), kind=kOutput, calls=%fused_computation.27 | convolution fusion | flops 270786560 | bytes 4227076 | tf_op jit(solution)/shard_map/dot_general | solution.py:81
  62.5 1.9 %collective-permute-start.3 = (s32[16,512]{1,0:T(8,128)S(1)}, s32[16,512]{1,0:T(8,128)S(1)}, u32[]{:S(2)}, u32[]{:S(2)}) collective-permute-start(s32[16,512]{1,0:T(8,128)S(1)} %get-tuple-element.24), channel_id=1, source_target_pairs={{0,1},{1,2},{2,3},{3,4},{4,5},{5,6},{6,7},{7,8},{8,9},{9,10},{10,1... | collective-permute-start | bytes 98312 | tf_op jit(solution)/shard_map/ppermute | solution.py:13
  64.4 3.8 %rev.23 = s32[256,512]{1,0:T(8,128)S(1)} reverse(s32[256,512]{1,0:T(8,128)} %get-tuple-element.11), dimensions={0,1} | reverse | bytes 1048576 | tf_op jit(solution)/shard_map/rev | solution.py:64
  68.2 2.1 %pad_add_fusion.2 = s32[512,512]{1,0:T(8,128)} fusion(s32[256,512]{1,0:T(8,128)S(1)} %rev.23, s32[256,512]{1,0:T(8,128)} %get-tuple-element.10), kind=kLoop, calls=%fused_computation.23 | loop fusion | flops 262144 | bytes 2097152 | tf_op jit(solution)/shard_map/concatenate | solution.py:65
  70.3 2.5 %copy.13 = s32[512,512]{0,1:T(8,128)} copy(s32[512,512]{1,0:T(8,128)} %pad_add_fusion.2) | data formatting | bytes 2097152 | tf_op jit(solution)/shard_map/concatenate | solution.py:65
  72.8 0.4 fusion.49
  73.3 0.6 copy-done
  73.9 0.3 copy-done.3
  74.2 1.5 %convert_multiply_fusion = (f32[512,512]{1,0:T(8,128)}, f32[512,512]{1,0:T(8,128)S(1)}) fusion(bf16[512,512]{1,0:T(8,128)(2,1)S(1)} %get-tuple-element.25, f32[]{:T(128)} %bitcast.4, f32[512,512]{1,0:T(8,128)S(1)} %fusion.49, s32[512,512]{0,1:T(8,128)S(1)} %copy-done.3, s32[256,512]{1,0:T(8,128)S(1)} %rev.23, s32[256,512]{1,0:T(8,128)S(1)} %copy-done), kind=kOutput, calls=%fused_computation.48 | convolution fusion | flops 270532608 | bytes 5767172 | tf_op jit(solution)/shard_map/dot_general | solution.py:81
  75.7 1.5 %convert_reduce_fusion.4 = (s32[]{:T(128)}, s32[]{:T(128)}, s32[]{:T(128)}) fusion(bf16[512,512]{1,0:T(8,128)(2,1)S(1)} %get-tuple-element.21, s32[512]{0:T(512)S(1)} %shift_right_arithmetic.162, s32[16,512]{1,0:T(8,128)S(1)} %and.71, bf16[512,512]{1,0:T(8,128)(2,1)S(1)} %get-tuple-element.25, f32[512,512]{1,0:T(8,128)S(1)} %get-tuple-element.23, f32[]{:T(128)} %bitcast.4), kind=kLoop, calls=%fused_computation.46 | loop fusion | flops 4718589 | bytes 2131984 | tf_op jit(solution)/shard_map/reduce_sum | solution.py:101
  77.2 0.0 collective-permute-done.3
  77.2 0.5 convolution_bitcast_fusion.1
  77.7 0.4 convolution_add_fusion.2
  78.1 1.5 %convert_multiply_fusion.1 = (f32[512,512]{1,0:T(8,128)}, f32[512,512]{1,0:T(8,128)S(1)}) fusion(bf16[512,512]{1,0:T(8,128)(2,1)S(1)} %fusion.6, f32[]{:T(128)} %bitcast.4, f32[512,512]{1,0:T(8,128)S(1)} %convolution_add_fusion.2, bf16[512,512]{1,0:T(8,128)(2,1)S(1)} %get-tuple-element.25), kind=kOutput, calls=%fused_computation.49 | convolution fusion | flops 269746176 | bytes 4194308 | tf_op jit(solution)/shard_map/dot_general | solution.py:74
  79.6 1.4 %convert_reduce_fusion.5 = (s32[]{:T(128)}, s32[]{:T(128)}, s32[]{:T(128)}) fusion(bf16[512,512]{1,0:T(8,128)(2,1)S(1)} %get-tuple-element.17, bf16[512,512]{1,0:T(8,128)(2,1)S(1)} %fusion.7, bf16[512,512]{1,0:T(8,128)(2,1)S(1)} %fusion.6, f32[512,512]{1,0:T(8,128)S(1)} %get-tuple-element.27, f32[]{:T(128)} %bitcast.4), kind=kLoop, calls=%fused_computation.47 | loop fusion | flops 2883581 | bytes 2621456 | tf_op jit(solution)/shard_map/reduce_sum | solution.py:100
  90.4 0.1 pad_add_fusion.3
  90.5 7.0 %psum.28 = s32[3]{0:T(128)S(1)} all-reduce(s32[3]{0:T(128)S(1)} %pad_add_fusion.3), channel_id=1, replica_groups=mesh['rows_0'=8,'rows_1'=8,'rows_2'=4,'rows_3'=2] {'rows_0'}, use_global_device_ids=true, to_apply=%region_12.13 | all-reduce | flops 3 | bytes 24 | tf_op jit(solution)/shard_map/psum | solution.py:18
  97.5 7.0 %psum.29 = s32[3]{0:T(128)S(1)} all-reduce(s32[3]{0:T(128)S(1)} %psum.28), channel_id=1, replica_groups=mesh['rows_0'=8,'rows_1'=8,'rows_2'=4,'rows_3'=2] {'rows_1'}, use_global_device_ids=true, to_apply=%region_13.14 | all-reduce | flops 3 | bytes 24 | tf_op jit(solution)/shard_map/psum | solution.py:18
  104.5 11.6 %psum.30 = s32[3]{0:T(128)S(1)} all-reduce(s32[3]{0:T(128)S(1)} %psum.29), channel_id=1, replica_groups=mesh['rows_0'=8,'rows_1'=8,'rows_2'=4,'rows_3'=2] {'rows_2'}, use_global_device_ids=true, to_apply=%region_14.15 | all-reduce | flops 3 | bytes 24 | tf_op jit(solution)/shard_map/psum | solution.py:18
  116.1 9.4 %psum.31 = s32[3]{0:T(128)} all-reduce(s32[3]{0:T(128)S(1)} %psum.30), channel_id=1, replica_groups=mesh['rows_0'=8,'rows_1'=8,'rows_2'=4,'rows_3'=2] {'rows_3'}, use_global_device_ids=true, to_apply=%region_15.16 | all-reduce | flops 3 | bytes 24 | tf_op jit(solution)/shard_map/psum | solution.py:18
  125.5 2.8 %pad_maximum_fusion = f32[512,1024]{1,0:T(8,128)} fusion(f32[512,512]{1,0:T(8,128)} %get-tuple-element.22, f32[512,512]{1,0:T(8,128)S(1)} %copy-done.2), kind=kLoop, calls=%fused_computation | loop fusion | flops 524288 | bytes 4194304 | tf_op jit(solution)/shard_map/concatenate | solution.py:121
  (13 shorter events, 0.1 us)
Async XLA Ops:
  0.6 1.4 %copy-start.4 = (s32[16,512]{1,0:T(8,128)S(1)}, s32[16,512]{1,0:T(8,128)}, u32[]{:S(2)}) copy-start(s32[16,512]{1,0:T(8,128)} %param.6) | copy-start | bytes 98308
  0.6 1.4 %copy-start.5 = (s32[16,512]{1,0:T(8,128)S(1)}, s32[16,512]{1,0:T(8,128)}, u32[]{:S(2)}) copy-start(s32[16,512]{1,0:T(8,128)} %param.8) | copy-start | bytes 98308
  3.5 13.2 %collective-permute-start.1 = (s32[8,512]{1,0:T(8,128)S(1)}, s32[8,512]{1,0:T(8,128)S(1)}, u32[]{:S(2)}, u32[]{:S(2)}) collective-permute-start(s32[8,512]{1,0:T(8,128)S(1)} %fusion.25), channel_id=1, source_target_pairs={{0,511},{1,0},{2,1},{3,2},{4,3},{5,4},{6,5},{7,6},{8,7},{9,8},{10,... | collective-permute-start | bytes 49160 | tf_op jit(solution)/shard_map/ppermute | solution.py:13
  12.6 12.8 %collective-permute-start = (s32[16,512]{1,0:T(8,128)S(1)}, s32[16,512]{1,0:T(8,128)S(1)}, u32[]{:S(2)}, u32[]{:S(2)}) collective-permute-start(s32[16,512]{1,0:T(8,128)S(1)} %get-tuple-element.9), channel_id=1, source_target_pairs={{0,1},{1,2},{2,3},{3,4},{4,5},{5,6},{6,7},{7,8},{8,9},{9,10},{10,1... | collective-permute-start | bytes 98312 | tf_op jit(solution)/shard_map/ppermute | solution.py:13
  23.5 14.6 %collective-permute-start.4 = (s32[16,512]{1,0:T(8,128)S(1)}, s32[16,512]{1,0:T(8,128)S(1)}, u32[]{:S(2)}, u32[]{:S(2)}) collective-permute-start(s32[16,512]{1,0:T(8,128)S(1)} %get-tuple-element.20), channel_id=1, source_target_pairs={{0,1},{1,2},{2,3},{3,4},{4,5},{5,6},{6,7},{7,8},{8,9},{9,10},{10,1... | collective-permute-start | bytes 98312 | tf_op jit(solution)/shard_map/ppermute | solution.py:13
  28.0 23.1 %collective-permute-start.2 = (s32[8,512]{1,0:T(8,128)S(1)}, s32[8,512]{1,0:T(8,128)S(1)}, u32[]{:S(2)}, u32[]{:S(2)}) collective-permute-start(s32[8,512]{1,0:T(8,128)S(1)} %fusion.24), channel_id=1, source_target_pairs={{0,511},{1,0},{2,1},{3,2},{4,3},{5,4},{6,5},{7,6},{8,7},{9,8},{10,... | collective-permute-start | bytes 49160 | tf_op jit(solution)/shard_map/ppermute | solution.py:13
  40.6 10.5 %collective-permute-start.5 = (s32[8,512]{1,0:T(8,128)S(1)}, s32[8,512]{1,0:T(8,128)S(1)}, u32[]{:S(2)}, u32[]{:S(2)}) collective-permute-start(s32[8,512]{1,0:T(8,128)S(1)} %fusion.23), channel_id=1, source_target_pairs={{0,511},{1,0},{2,1},{3,2},{4,3},{5,4},{6,5},{7,6},{8,7},{9,8},{10,... | collective-permute-start | bytes 49160 | tf_op jit(solution)/shard_map/ppermute | solution.py:13
  52.5 5.0 %copy-start.1 = (s32[256,512]{1,0:T(8,128)}, s32[256,512]{1,0:T(8,128)S(1)}, u32[]{:S(2)}) copy-start(s32[256,512]{1,0:T(8,128)S(1)} %get-tuple-element.19) | copy-start | bytes 1572868
  62.5 14.7 %collective-permute-start.3 = (s32[16,512]{1,0:T(8,128)S(1)}, s32[16,512]{1,0:T(8,128)S(1)}, u32[]{:S(2)}, u32[]{:S(2)}) collective-permute-start(s32[16,512]{1,0:T(8,128)S(1)} %get-tuple-element.24), channel_id=1, source_target_pairs={{0,1},{1,2},{2,3},{3,4},{4,5},{5,6},{6,7},{7,8},{8,9},{9,10},{10,1... | collective-permute-start | bytes 98312 | tf_op jit(solution)/shard_map/ppermute | solution.py:13
  72.8 1.0 copy-start
  72.8 1.4 %copy-start.3 = (s32[512,512]{0,1:T(8,128)S(1)}, s32[512,512]{0,1:T(8,128)}, u32[]{:S(2)}) copy-start(s32[512,512]{0,1:T(8,128)} %copy.13) | copy-start | bytes 3145732
  79.6 45.9 %copy-start.2 = (f32[512,512]{1,0:T(8,128)S(1)}, f32[512,512]{1,0:T(8,128)}, u32[]{:S(2)}) copy-start(f32[512,512]{1,0:T(8,128)} %get-tuple-element.26) | copy-start | bytes 3145732
where the time goes:
time: 129 us; the launch traced here: 128 us
  blocking collectives  35 us (27%)
  starting transfers between devices  33.7 us (26%)
  local copies, waits for them, and re-layouts  20.4 us (16%)
  matrix products  14.6 us (11%)
  other arithmetic  13.6 us (11%)
  between operations  11.1 us (9%)
    psum x4, blocking collectives, over_axes(): array = lax.psum(array, axis)  35 us
    ppermute x6, starting transfers between devices, shifted(): lax.ppermute(array, axis, [(i, (i + by) % count) for i in range(count)])  33.7 us
    rev x3, local copies, waits for them, and re-layouts, unfold_within(): jnp.where(col_ids < row_ids, folded, jnp.zeros_like(folded))[::-1, ::-1]  8.42 us
    concatenate x3, local copies, waits for them, and re-layouts, unfold_within(): upper_half = jnp.concatenate([top_rows, bottom_rows], axis=0)  7.69 us
    dot_general x3, matrix products, support_across(): jnp.dot(across, next_within, preferred_element_type=jnp.float32)  6.13 us
    concatenate x3, other arithmetic, unfold_within(): upper_half = jnp.concatenate([top_rows, bottom_rows], axis=0)  4.27 us
    dot_general x3, matrix products, support_across(): between = jnp.dot(within, across, preferred_element_type=jnp.float32)  3.25 us
    concatenate x1, other arithmetic, on_device(): jnp.concatenate([inside * within.astype(jnp.float32), between * across.as...  2.76 us
  transfers between devices with their start and end apart: 6, of which 0 were waited for; matrix products, arithmetic and copies ran while one was open for 21% of the time, Pallas kernels for 0%

commit v1 on v0

v1 whole, which is shorter than its diff:
```python
import jax
import jax.numpy as jnp
from jax import lax
from jax.experimental import pallas as pl
from jax.experimental.pallas import tpu as pltpu
from jax.sharding import PartitionSpec as P

TILE = 512
WORDS = TILE // 32
HALF = 4
F8 = jnp.float8_e4m3fn
F32 = jnp.float32
I32 = jnp.int32
MESH = pl.DeviceIdType.MESH
CORE, XAX, YAX, ZAX = (1, 2), (2, 4), (8, 8), (64, 8)
PHASES = ((CORE,), (XAX,), (YAX,), (ZAX,))


def rows_index():
    return lax.axis_index("rows")


def signal(sem, device):
    pl.semaphore_signal(sem, inc=1, device_id=(device,), device_id_type=MESH)


def exchange_kernel(n, ad, ar, ld, lr, acr, wit, send_sem, recv_sem):
    me = rows_index()
    barrier = pltpu.get_barrier_semaphore()
    dev = {k: lax.rem(me + k + n, n) for k in (-2, -1, 1, 2)}
    for k in dev:
        signal(barrier, dev[k])
    acr[2] = ar[...] & lr[...]
    wit[1] = ad[...] & ld[...]
    pl.semaphore_wait(barrier, 4)
    plan = (
        (acr, 2, 1, 1), (wit, 1, -1, 2), (acr, 2, -1, 3), (wit, 1, 1, 0),
        (acr, 2, 2, 0), (wit, 1, -2, 3),
    )
    copies = []
    for i, (ref, src, to, dst) in enumerate(plan):
        copies.append(
            pltpu.make_async_remote_copy(
                src_ref=ref.at[src], dst_ref=ref.at[dst],
                send_sem=send_sem.at[i], recv_sem=recv_sem.at[i],
                device_id=(dev[to],), device_id_type=MESH,
            )
        )
        copies[-1].start()
    for c in copies:
        c.wait_recv()
    for c in copies:
        c.wait_send()


def peer_list(me, phase):
    offsets = [0]
    ids = [me]
    for stride, size in phase:
        pos = lax.rem(lax.div(me, stride), size)
        new = []
        for base in ids:
            for k in range(size):
                other = lax.rem(pos + k, size)
                new.append(base + (other - pos) * stride)
        ids = new
    return ids[1:]


def dot(a, b):
    return jnp.dot(a, b, preferred_element_type=F32)


def dot_tn(a, b):
    return lax.dot_general(a, b, (((0,), (0,)), ((), ())), preferred_element_type=F32)


def dot_nt(a, b):
    return lax.dot_general(a, b, (((1,), (1,)), ((), ())), preferred_element_type=F32)


def unpack(words):
    bit = lax.broadcasted_iota(I32, (32, TILE), 0)
    return (words >> bit) & 1


def peel_kernel(th_ref, acr, wit, sup, cnt_ref, A, W, U, sbuf, rbuf, send_sem, recv_sem):
    me = rows_index()
    barrier = pltpu.get_barrier_semaphore()
    peers = [peer_list(me, p) for p in PHASES]
    for group in peers:
        for d in group:
            signal(barrier, d)
    thresh = (th_ref[0] - 2).astype(F32)

    def open_across(t, _):
        for g in range(WORDS):
            A[0, t, 32 * g:32 * g + 32, :] = unpack(acr[t, g:g + 1, :]).astype(F32).astype(F8)
        return 0

    def open_within(t, _):
        for g in range(WORDS):
            r = lax.broadcasted_iota(I32, (32, TILE), 0) + 32 * g
            c = lax.broadcasted_iota(I32, (32, TILE), 1)
            U[32 * g:32 * g + 32, :] = jnp.where(c > r, unpack(wit[t, g:g + 1, :]), 0).astype(F32)
        u = U[...]
        W[0, t] = (u + u.T).astype(F8)
        return 0

    lax.fori_loop(0, HALF, open_across, 0)
    lax.fori_loop(0, HALF, open_within, 0)

    def inside(s, j):
        return (
            dot_tn(A[s, j], A[s, j]) + dot(W[s, j], W[s, j]) + dot_nt(A[s, j + 1], A[s, j + 1])
        )

    def between(s, j):
        return dot(W[s, j], A[s, j + 1]) + dot(A[s, j + 1], W[s, j + 1])

    def keep(x, old):
        return jnp.where(x >= thresh, old.astype(F32), 0.0)

    def edges(w, a):
        s = jnp.sum(w, axis=0, keepdims=True) * 0.5 + jnp.sum(a, axis=0, keepdims=True)
        return jnp.sum(s, axis=1, keepdims=True)

    def held(s):
        return edges(W[s, 1].astype(F32), A[s, 2].astype(F32))

    total = [held(0)]
    for j in range(3):
        W[1, j] = keep(inside(0, j), W[0, j]).astype(F8)
        A[1, j + 1] = keep(between(0, j), A[0, j + 1]).astype(F8)
    total.append(held(1))
    for j in range(2):
        A[0, j + 1] = keep(between(1, j), A[1, j + 1]).astype(F8)
        W[0, j + 1] = keep(inside(1, j + 1), W[1, j + 1]).astype(F8)
    total.append(held(0))
    x = inside(0, 1)
    w = keep(x, W[0, 1])
    sup[:, :TILE] = x * w
    x = between(0, 1)
    a = keep(x, A[0, 2])
    sup[:, TILE:] = x * a
    total.append(edges(w, a))

    lane = lax.broadcasted_iota(I32, (1, 128), 1)
    acc = jnp.zeros((1, 128), I32)
    for i in range(3):
        lost = (total[i] - total[i + 1]).astype(I32)
        acc = jnp.where(lane == i, lost, acc)

    pl.semaphore_wait(barrier, sum(len(g) for g in peers))
    sends = []
    for p, group in enumerate(peers):
        sbuf[p:p + 1, :] = acc
        copies = []
        for k, d in enumerate(group):
            copies.append(
                pltpu.make_async_remote_copy(
                    src_ref=sbuf.at[pl.ds(p, 1)], dst_ref=rbuf.at[p, pl.ds(k, 1)],
                    send_sem=send_sem.at[p, k], recv_sem=recv_sem.at[p, k],
                    device_id=(d,), device_id_type=MESH,
                )
            )
            copies[-1].start()
        for c in copies:
            c.wait_recv()
        for k in range(len(group)):
            acc = acc + rbuf[p, k:k + 1, :]
        sends += copies
    cnt_ref[...] = acc
    for c in sends:
        c.wait_send()


def on_device(adj_diag, adj_right, alive_diag, alive_right, truss_k):
    n = lax.axis_size("rows")
    vmem = pl.BlockSpec(memory_space=pltpu.VMEM)
    words = jax.ShapeDtypeStruct((HALF, WORDS, TILE), I32)
    acr, wit = pl.pallas_call(
        lambda *refs: exchange_kernel(n, *refs),
        out_shape=(words, words),
        in_specs=[vmem] * 4,
        out_specs=[vmem] * 2,
        scratch_shapes=[pltpu.SemaphoreType.DMA((6,)), pltpu.SemaphoreType.DMA((6,))],
        compiler_params=pltpu.CompilerParams(collective_id=0, has_side_effects=True),
        name="exchange",
    )(adj_diag, adj_right, alive_diag, alive_right)
    most = max(len_of(p) for p in PHASES)
    support, counts = pl.pallas_call(
        peel_kernel,
        out_shape=(
            jax.ShapeDtypeStruct((TILE, 2 * TILE), F32),
            jax.ShapeDtypeStruct((1, 128), I32),
        ),
        in_specs=[pl.BlockSpec(memory_space=pltpu.SMEM), vmem, vmem],
        out_specs=[vmem, vmem],
        scratch_shapes=[
            pltpu.VMEM((2, HALF, TILE, TILE), F8),
            pltpu.VMEM((2, HALF, TILE, TILE), F8),
            pltpu.VMEM((TILE, TILE), F32),
            pltpu.VMEM((len(PHASES), 128), I32),
            pltpu.VMEM((len(PHASES), most, 128), I32),
            pltpu.SemaphoreType.DMA((len(PHASES), most)),
            pltpu.SemaphoreType.DMA((len(PHASES), most)),
        ],
        compiler_params=pltpu.CompilerParams(
            collective_id=1, has_side_effects=True, vmem_limit_bytes=56 * 2**20
        ),
        name="peel",
    )(truss_k, acr, wit)
    return support, counts[0, :3]


def len_of(phase):
    size = 1
    for _, s in phase:
        size *= s
    return size - 1


def solution(mesh):
    rows = P("rows", None)
    return jax.shard_map(
        on_device, mesh=mesh, in_specs=(rows, rows, rows, rows, P(None)),
        out_specs=(rows, P(None)), check_vma=False,
    )
```

time: 129 us -> 48 us (0.37)
  Pallas kernels: 0 us -> 41.6 us
  blocking collectives: 35 us -> 0 us
  starting transfers between devices: 33.7 us -> 0 us
  local copies, waits for them, and re-layouts: 20.4 us -> 4.35 us
  matrix products: 14.6 us -> 0 us
  other arithmetic: 13.6 us -> 0 us
  between operations: 11.1 us -> 1.29 us
    pallas_call x0 -> x2, Pallas kernels: none -> 41.6 us  [the longest x1 21.6 us: on_device(): pl.pallas_call(peel_kernel, out_shape=(jax.ShapeDtypeStruct((TILE, 2 * TI...]
    psum x4 -> x0, blocking collectives: 35 us -> none  [over_axes(): array = lax.psum(array, axis)]
    ppermute x6 -> x0, starting transfers between devices: 33.7 us -> none  [shifted(): lax.ppermute(array, axis, [(i, (i + by) % count) for i in range(count)])]
    dot_general x15 -> x0, matrix products: 14.6 us -> none  [the longest x3 6.13 us: support_across(): jnp.dot(across, next_within, preferred_element_type=jnp.float32)]
    rev x6 -> x0, local copies, waits for them, and re-layouts: 11.1 us -> none  [the longest x3 8.42 us: unfold_within(): jnp.where(col_ids < row_ids, folded, jnp.zeros_like(folded))[::-1, ::-1]]
    concatenate x3 -> x0, local copies, waits for them, and re-layouts: 7.69 us -> none  [unfold_within(): upper_half = jnp.concatenate([top_rows, bottom_rows], axis=0)]
    concatenate x4 -> x0, other arithmetic: 7.04 us -> none  [the longest x3 4.27 us: unfold_within(): upper_half = jnp.concatenate([top_rows, bottom_rows], axis=0)]
    reduce_sum x5 -> x0, other arithmetic: 3.26 us -> none  [the longest x1 1.48 us: tally(): removed = removed + jnp.sum((across - new_across).astype(jnp.int32))]
  transfers between devices with their start and end apart: 6 -> 0, of which waited for: 0 -> 0; matrix products, arithmetic and copies ran while one was open for 21% -> 0% of each run, Pallas kernels for 0% -> 0%
where the time goes in v1:
time: 48 us; the launch traced here: 47.2 us
  Pallas kernels  41.6 us (87%)
  local copies, waits for them, and re-layouts  4.35 us (9%)
  between operations  1.29 us (3%)
    pallas_call x1, Pallas kernels, on_device(): pl.pallas_call(peel_kernel, out_shape=(jax.ShapeDtypeStruct((TILE, 2 * TI...  21.6 us
    pallas_call x1, Pallas kernels, on_device(): pl.pallas_call(lambda *refs: exchange_kernel(n, *refs), out_shape=(words,...  20 us
    unnamed x1, local copies, waits for them, and re-layouts  3.16 us
    squeeze x1, local copies, waits for them, and re-layouts, on_device(): return (support, counts[0, :3])  1.19 us

profile of v1, /device:TPU:1, one launch (start us, length us, event | category | flops | bytes accessed | tf_op | source)
XLA Modules:
  0.0 47.2 jit_solution(14183214770921547047)
XLA Ops:
  1.3 20.0 %exchange.1 = (s32[4,16,512]{2,1,0:T(8,128)}, s32[4,16,512]{2,1,0:T(8,128)}) custom-call(s32[16,512]{1,0:T(8,128)} %refs_0_.1, s32[16,512]{1,0:T(8,128)} %refs_1_.1, s32[16,512]{1,0:T(8,128)} %refs_2_.1, s32[16,512]{1,0:T(8,128)} %refs_3_.1), custom_call_target="tpu_custom_call" | custom-call | tf_op jit(solution)/shard_map/exchange/pallas_call | solution.py:182
  21.3 21.6 %peel.1 = (f32[512,1024]{1,0:T(8,128)}, s32[1,128]{1,0:T(1,128)}) custom-call(s32[1]{0:T(128)S(6)} %copy.8.th_ref, s32[4,16,512]{2,1,0:T(8,128)} %get-tuple-element.6.acr, s32[4,16,512]{2,1,0:T(8,128)} %get-tuple-element.7.wit), custom_call_target="tpu_custom_call" | custom-call | tf_op jit(solution)/shard_map/peel/pallas_call | solution.py:192
  42.9 1.2 %slice_bitcast_fusion = s32[3]{0:T(128)} fusion(s32[1,128]{1,0:T(1,128)} %get-tuple-element.9), kind=kLoop, calls=%fused_computation | loop fusion | bytes 24 | tf_op jit(solution)/shard_map/squeeze | solution.py:214
  44.1 3.2 %copy.9 = f32[512,1024]{1,0:T(8,128)} copy(f32[512,1024]{1,0:T(8,128)} %get-tuple-element.12) | data formatting | bytes 4194304

commit v2 on v1

v2 whole, which is shorter than its diff:
```python
import jax
import jax.numpy as jnp
from jax import lax
from jax.experimental import pallas as pl
from jax.experimental.pallas import tpu as pltpu
from jax.sharding import PartitionSpec as P

TILE = 512
WORDS = TILE // 32
HALF = 4
F8 = jnp.float8_e4m3fn
F32 = jnp.float32
I32 = jnp.int32
MESH = pl.DeviceIdType.MESH
XAX, YAX, ZAX = (2, 4), (8, 8), (64, 8)
GATHER = (YAX,)
SPREAD = (XAX, ZAX)


def chips_of(chip, axes):
    ids = [chip]
    for stride, size in axes:
        pos = lax.rem(lax.div(chip, stride), size)
        ids = [
            base + (lax.rem(pos + k, size) - pos) * stride if k else base
            for base in ids for k in range(size)
        ]
    return ids


def dot(a, b):
    return jnp.dot(a, b, preferred_element_type=F32)


def dot_tn(a, b):
    return lax.dot_general(a, b, (((0,), (0,)), ((), ())), preferred_element_type=F32)


def dot_nt(a, b):
    return lax.dot_general(a, b, (((1,), (1,)), ((), ())), preferred_element_type=F32)


def unpack(words):
    bit = lax.broadcasted_iota(I32, (32, TILE), 0)
    return (words >> bit) & 1


def peel_kernel(
    n, ad, ar, ld, lr, th_ref, sup, cnt_ref,
    raw, acr, wit, A, W, U, Pw, Qa, sbuf, rbuf,
    in_sem, x_send, x_recv, r_send, r_recv,
):
    me = lax.axis_index("rows")
    core = lax.rem(me, 2)
    chip = me - core
    mate = chip + 1 - core
    gather = chips_of(chip, GATHER)
    spread = chips_of(chip, SPREAD)
    dev = {k: lax.rem(me + k + n, n) for k in (-2, -1, 1, 2)}

    loads = [
        pltpu.make_async_copy(src, raw.at[i], in_sem.at[i])
        for i, src in enumerate((ar, lr, ad, ld))
    ]
    for c in loads:
        c.start()

    barrier = pltpu.get_barrier_semaphore()

    def signal(device):
        pl.semaphore_signal(barrier, inc=1, device_id=(device,), device_id_type=MESH)

    for k in dev:
        signal(dev[k])

    signal(mate)
    for c in gather[1:] + spread[1:]:
        signal(c + 1)

    @pl.when(core == 1)
    def _():
        for c in gather[1:] + spread[1:]:
            signal(c)

    loads[0].wait()
    loads[1].wait()
    acr[2] = raw[0] & raw[1]
    loads[2].wait()
    loads[3].wait()
    wit[1] = raw[2] & raw[3]
    even_count = 4 + len(gather) + len(spread) - 1

    @pl.when(core == 0)
    def _():
        pl.semaphore_wait(barrier, even_count)

    @pl.when(core == 1)
    def _():
        pl.semaphore_wait(barrier, even_count + len(gather) + len(spread) - 2)

    plan = (
        (acr, 2, 1, 1), (wit, 1, -1, 2), (wit, 1, 1, 0), (acr, 2, -1, 3),
        (acr, 2, 2, 0), (wit, 1, -2, 3),
    )
    moves = []
    for i, (ref, src, to, dst) in enumerate(plan):
        moves.append(
            pltpu.make_async_remote_copy(
                src_ref=ref.at[src], dst_ref=ref.at[dst],
                send_sem=x_send.at[i], recv_sem=x_recv.at[i],
                device_id=(dev[to],), device_id_type=MESH,
            )
        )
        moves[-1].start()

    thresh = (th_ref[0] - 2).astype(F32)

    def open_across(t):
        for g in range(WORDS):
            A[0, t, 32 * g:32 * g + 32, :] = unpack(acr[t, g:g + 1, :]).astype(F32).astype(F8)

    def open_within(t):
        for g in range(WORDS):
            r = lax.broadcasted_iota(I32, (32, TILE), 0) + 32 * g
            c = lax.broadcasted_iota(I32, (32, TILE), 1)
            U[32 * g:32 * g + 32, :] = jnp.where(c > r, unpack(wit[t, g:g + 1, :]), 0).astype(F32)
        u = U[...]
        W[0, t] = (u + u.T).astype(F8)

    def keep(x, old):
        return jnp.where(x >= thresh, old.astype(F32), 0.0)

    def edges(w, a):
        s = jnp.sum(w, axis=0, keepdims=True) * 0.5 + jnp.sum(a, axis=0, keepdims=True)
        return jnp.sum(s, axis=1, keepdims=True)

    def inside(s, j):
        return (
            dot_tn(A[s, j], A[s, j]) + dot(W[s, j], W[s, j]) + dot_nt(A[s, j + 1], A[s, j + 1])
        )

    def between(s, j):
        return dot(W[s, j], A[s, j + 1]) + dot(A[s, j + 1], W[s, j + 1])

    open_across(2)
    open_within(1)
    a = A[0, 2]
    w = W[0, 1]
    total = [edges(w.astype(F32), a.astype(F32))]
    Pw[...] = dot(w, w) + dot_nt(a, a)
    Qa[...] = dot(w, a)

    for c in moves[:4]:
        c.wait_recv()
    open_across(1)
    open_within(2)
    open_within(0)
    open_across(3)
    w = keep(dot_tn(A[0, 1], A[0, 1]) + Pw[...], W[0, 1])
    W[1, 1] = w.astype(F8)
    a = keep(dot(A[0, 2], W[0, 2]) + Qa[...], A[0, 2])
    A[1, 2] = a.astype(F8)
    total.append(edges(w, a))
    A[1, 1] = keep(between(0, 0), A[0, 1]).astype(F8)
    W[1, 2] = keep(inside(0, 2), W[0, 2]).astype(F8)

    for c in moves[4:]:
        c.wait_recv()
    open_across(0)
    open_within(3)
    W[1, 0] = keep(inside(0, 0), W[0, 0]).astype(F8)
    A[1, 3] = keep(between(0, 2), A[0, 3]).astype(F8)

    A[0, 1] = keep(between(1, 0), A[1, 1]).astype(F8)
    W[0, 2] = keep(inside(1, 2), W[1, 2]).astype(F8)
    w = keep(inside(1, 1), W[1, 1])
    W[0, 1] = w.astype(F8)
    a = keep(between(1, 1), A[1, 2])
    A[0, 2] = a.astype(F8)
    total.append(edges(w, a))

    x = inside(0, 1)
    sup[:, :TILE] = x
    w = keep(x, W[0, 1])
    y = between(0, 1)
    sup[:, TILE:] = y
    a = keep(y, A[0, 2])
    total.append(edges(w, a))

    lane = lax.broadcasted_iota(I32, (1, 128), 1)
    acc = jnp.zeros((1, 128), I32)
    for i in range(3):
        lost = (total[i] - total[i + 1]).astype(I32)
        acc = jnp.where(lane == i, lost, acc)
    sbuf[0:1, :] = acc
    rbuf[0, 1:2, :] = acc

    def send(stage, slot, device, k):
        return pltpu.make_async_remote_copy(
            src_ref=sbuf.at[pl.ds(stage, 1)], dst_ref=rbuf.at[stage, pl.ds(slot, 1)],
            send_sem=r_send.at[stage, k], recv_sem=r_recv.at[stage, slot],
            device_id=(device,), device_id_type=MESH,
        )

    far = range(len(gather) - 1, -1, -1)

    @pl.when(core == 0)
    def _():
        for k in far:
            send(0, 2 * k, gather[k] + 1, k).start()

    @pl.when(core == 1)
    def _():
        for k in far[:-1]:
            send(0, 2 * k + 1, gather[k] + 1, k).start()

    sup[:, :TILE] = sup[:, :TILE] * jnp.where(
        sup[:, :TILE] >= thresh, W[0, 1].astype(F32), 0.0)
    sup[:, TILE:] = sup[:, TILE:] * jnp.where(
        sup[:, TILE:] >= thresh, A[0, 2].astype(F32), 0.0)

    @pl.when(core == 1)
    def _():
        for k in range(len(gather)):
            for c in (0, 1):
                if k or not c:
                    send(0, 2 * k + c, mate, k).wait_recv()
        part = jnp.sum(rbuf[0, 0:2 * len(gather), :], axis=0, keepdims=True)
        sbuf[1:2, :] = part
        rbuf[1, 0:1, :] = part
        count = len(spread)
        for k in range(count - 1, -1, -1):
            if k:
                send(1, k, spread[k] + 1, k).start()
            send(1, k, spread[k], count + k).start()
        for k in range(1, count):
            send(1, k, mate, k).wait_recv()

    @pl.when(core == 0)
    def _():
        for k in range(len(spread)):
            send(1, k, mate, k).wait_recv()

    cnt_ref[...] = jnp.sum(rbuf[1, 0:len(spread), :], axis=0, keepdims=True)

    for c in moves:
        c.wait_send()

    @pl.when(core == 0)
    def _():
        for k in far:
            send(0, 2 * k, mate, k).wait_send()

    @pl.when(core == 1)
    def _():
        for k in far[:-1]:
            send(0, 2 * k + 1, mate, k).wait_send()
        for k in range(2 * len(spread)):
            if k:
                send(1, 0, mate, k).wait_send()


def write_kernel(sup, cnt, out, counts, sem):
    copies = [
        pltpu.make_async_copy(sup.at[pl.ds(128 * i, 128)], out.at[pl.ds(128 * i, 128)], sem.at[i])
        for i in range(4)
    ]
    for c in copies:
        c.start()
    counts[...] = cnt[0, :3]
    for c in copies:
        c.wait()


def group_size(axes):
    size = 1
    for _, s in axes:
        size *= s
    return size


def on_device(adj_diag, adj_right, alive_diag, alive_right, truss_k):
    n = lax.axis_size("rows")
    vmem = pl.BlockSpec(memory_space=pltpu.VMEM)
    smem = pl.BlockSpec(memory_space=pltpu.SMEM)
    hbm = pl.BlockSpec(memory_space=pl.ANY)
    slots = max(2 * group_size(GATHER), 2 * group_size(SPREAD))
    tiles = [
        pltpu.with_memory_space_constraint(x, pltpu.HBM)
        for x in (adj_diag, adj_right, alive_diag, alive_right)
    ]
    support, counts = pl.pallas_call(
        lambda *refs: peel_kernel(n, *refs),
        out_shape=(
            pltpu.VMEM((TILE, 2 * TILE), F32),
            pltpu.VMEM((1, 128), I32),
        ),
        in_specs=[pl.BlockSpec(memory_space=pltpu.HBM)] * 4 + [smem],
        out_specs=[vmem, vmem],
        scratch_shapes=[
            pltpu.VMEM((4, WORDS, TILE), I32),
            pltpu.VMEM((HALF, WORDS, TILE), I32),
            pltpu.VMEM((HALF, WORDS, TILE), I32),
            pltpu.VMEM((2, HALF, TILE, TILE), F8),
            pltpu.VMEM((2, HALF, TILE, TILE), F8),
            pltpu.VMEM((TILE, TILE), F32),
            pltpu.VMEM((TILE, TILE), F32),
            pltpu.VMEM((TILE, TILE), F32),
            pltpu.VMEM((2, 128), I32),
            pltpu.VMEM((2, slots, 128), I32),
            pltpu.SemaphoreType.DMA((4,)),
            pltpu.SemaphoreType.DMA((6,)),
            pltpu.SemaphoreType.DMA((6,)),
            pltpu.SemaphoreType.DMA((2, slots)),
            pltpu.SemaphoreType.DMA((2, slots)),
        ],
        compiler_params=pltpu.CompilerParams(
            collective_id=0, has_side_effects=True, vmem_limit_bytes=40 * 2**20
        ),
        name="peel",
    )(*tiles, truss_k)
    return pl.pallas_call(
        write_kernel,
        out_shape=(
            jax.ShapeDtypeStruct((TILE, 2 * TILE), F32),
            jax.ShapeDtypeStruct((3,), I32),
        ),
        in_specs=[vmem, vmem],
        out_specs=[hbm, vmem],
        scratch_shapes=[pltpu.SemaphoreType.DMA((4,))],
        compiler_params=pltpu.CompilerParams(vmem_limit_bytes=4 * 2**20),
        name="write",
    )(support, counts)


def solution(mesh):
    rows = P("rows", None)
    return jax.shard_map(
        on_device, mesh=mesh, in_specs=(rows, rows, rows, rows, P(None)),
        out_specs=(rows, P(None)), check_vma=False,
    )
```

time: 48 us -> 39.4 us (0.82); the launches traced: 47.2 us -> 39.2 us
  local copies, waits for them, and re-layouts: 4.35 us -> 0 us
  Pallas kernels: 41.6 us -> 37.9 us
    pallas_call x2, Pallas kernels: 41.6 us -> 37.9 us  [the longest x1 36 us: on_device(): pl.pallas_call(lambda *refs: peel_kernel(n, *refs), out_shape=(pltpu.VMEM...]
    unnamed x1 -> x0, local copies, waits for them, and re-layouts: 3.16 us -> none
    squeeze x1 -> x0, local copies, waits for them, and re-layouts: 1.19 us -> none  [on_device(): return (support, counts[0, :3])]
where the time goes in v2:
time: 39.4 us; the launch traced here: 39.2 us
  Pallas kernels  37.9 us (96%)
  between operations  1.29 us (3%)
    pallas_call x1, Pallas kernels, on_device(): pl.pallas_call(lambda *refs: peel_kernel(n, *refs), out_shape=(pltpu.VMEM...  36 us
    pallas_call x1, Pallas kernels, on_device(): pl.pallas_call(write_kernel, out_shape=(jax.ShapeDtypeStruct((TILE, 2 * T...  1.86 us

profile of v2, /device:TPU:1, one launch (start us, length us, event | category | flops | bytes accessed | tf_op | source)
XLA Modules:
  0.0 39.2 jit_solution(1703563957557482440)
XLA Ops:
  1.3 36.0 %peel.1 = (f32[512,1024]{1,0:T(8,128)S(1)}, s32[1,128]{1,0:T(1,128)S(1)}) custom-call(s32[16,512]{1,0:T(8,128)} %refs_0_.1, s32[16,512]{1,0:T(8,128)} %refs_1_.1, s32[16,512]{1,0:T(8,128)} %refs_2_.1, s32[16,512]{1,0:T(8,128)} %refs_3_.1, s32[1]{0:T(128)S(6)} %copy.7.refs_4_), custom_call_target="tpu_custom_call" | custom-call | tf_op jit(solution)/shard_map/peel/pallas_call | solution.py:292
  37.3 1.9 %write.1 = (f32[512,1024]{1,0:T(8,128)}, s32[3]{0:T(128)}) custom-call(f32[512,1024]{1,0:T(8,128)S(1)} %get-tuple-element.4.sup, s32[1,128]{1,0:T(1,128)S(1)} %get-tuple-element.5.cnt), custom_call_target="tpu_custom_call" | custom-call | tf_op jit(solution)/shard_map/write/pallas_call | solution.py:322

commit v3 on v2

--- a/solution.py
+++ b/solution.py
@@ -47,7 +47,7 @@
 
 def peel_kernel(
     n, ad, ar, ld, lr, th_ref, sup, cnt_ref,
-    raw, acr, wit, A, W, U, Pw, Qa, sbuf, rbuf,
+    raw, acr, wit, A, W, U, Pw, Qa, sbuf, buf1, buf2, buf3,
     in_sem, x_send, x_recv, r_send, r_recv,
 ):
     me = lax.axis_index("rows")
@@ -74,13 +74,15 @@
         signal(dev[k])
 
     signal(mate)
-    for c in gather[1:] + spread[1:]:
+    for c in gather[1:]:
         signal(c + 1)
 
     @pl.when(core == 1)
     def _():
-        for c in gather[1:] + spread[1:]:
+        for c in gather[1:]:
             signal(c)
+        for c in spread[1:]:
+            signal(c + 1)
 
     loads[0].wait()
     loads[1].wait()
@@ -88,7 +90,7 @@
     loads[2].wait()
     loads[3].wait()
     wit[1] = raw[2] & raw[3]
-    even_count = 4 + len(gather) + len(spread) - 1
+    even_count = 4 + len(gather)
 
     @pl.when(core == 0)
     def _():
@@ -150,27 +152,39 @@
     Pw[...] = dot(w, w) + dot_nt(a, a)
     Qa[...] = dot(w, a)
 
-    for c in moves[:4]:
-        c.wait_recv()
-    open_across(1)
-    open_within(2)
-    open_within(0)
-    open_across(3)
-    w = keep(dot_tn(A[0, 1], A[0, 1]) + Pw[...], W[0, 1])
-    W[1, 1] = w.astype(F8)
-    a = keep(dot(A[0, 2], W[0, 2]) + Qa[...], A[0, 2])
-    A[1, 2] = a.astype(F8)
-    total.append(edges(w, a))
-    A[1, 1] = keep(between(0, 0), A[0, 1]).astype(F8)
-    W[1, 2] = keep(inside(0, 2), W[0, 2]).astype(F8)
-
-    for c in moves[4:]:
-        c.wait_recv()
-    open_across(0)
-    open_within(3)
-    W[1, 0] = keep(inside(0, 0), W[0, 0]).astype(F8)
-    A[1, 3] = keep(between(0, 2), A[0, 3]).astype(F8)
-
+    def from_left():
+        for i in (0, 2, 4):
+            moves[i].wait_recv()
+        open_across(1)
+        open_within(0)
+        open_across(0)
+        W[1, 1] = keep(dot_tn(A[0, 1], A[0, 1]) + Pw[...], W[0, 1]).astype(F8)
+        A[1, 1] = keep(between(0, 0), A[0, 1]).astype(F8)
+        W[1, 0] = keep(inside(0, 0), W[0, 0]).astype(F8)
+
+    def from_right():
+        for i in (1, 3, 5):
+            moves[i].wait_recv()
+        open_within(2)
+        open_across(3)
+        open_within(3)
+        A[1, 2] = keep(dot(A[0, 2], W[0, 2]) + Qa[...], A[0, 2]).astype(F8)
+        W[1, 2] = keep(inside(0, 2), W[0, 2]).astype(F8)
+        A[1, 3] = keep(between(0, 2), A[0, 3]).astype(F8)
+
+    last_chip = lax.rem(lax.div(chip, XAX[0]), XAX[1]) == XAX[1] - 1
+
+    @pl.when(last_chip)
+    def _():
+        from_left()
+        from_right()
+
+    @pl.when(jnp.logical_not(last_chip))
+    def _():
+        from_right()
+        from_left()
+
+    total.append(edges(W[1, 1].astype(F32), A[1, 2].astype(F32)))
     A[0, 1] = keep(between(1, 0), A[1, 1]).astype(F8)
     W[0, 2] = keep(inside(1, 2), W[1, 2]).astype(F8)
     w = keep(inside(1, 1), W[1, 1])
@@ -192,82 +206,68 @@
     for i in range(3):
         lost = (total[i] - total[i + 1]).astype(I32)
         acc = jnp.where(lane == i, lost, acc)
+    near, wide = len(gather), len(spread)
     sbuf[0:1, :] = acc
-    rbuf[0, 1:2, :] = acc
-
-    def send(stage, slot, device, k):
+    buf1[2 * near - 1:2 * near, :] = acc
+
+    def send(stage, buf, row, count, device):
         return pltpu.make_async_remote_copy(
-            src_ref=sbuf.at[pl.ds(stage, 1)], dst_ref=rbuf.at[stage, pl.ds(slot, 1)],
-            send_sem=r_send.at[stage, k], recv_sem=r_recv.at[stage, slot],
+            src_ref=(sbuf if count == 1 else buf).at[pl.ds(stage if count == 1 else 0, count)],
+            dst_ref=buf.at[pl.ds(row, count)],
+            send_sem=r_send.at[stage], recv_sem=r_recv.at[stage],
             device_id=(device,), device_id_type=MESH,
         )
 
-    far = range(len(gather) - 1, -1, -1)
-
     @pl.when(core == 0)
     def _():
-        for k in far:
-            send(0, 2 * k, gather[k] + 1, k).start()
+        for k in range(near - 1, 0, -1):
+            send(0, buf1, 2 * k - 2, 1, gather[k] + 1).start()
+        send(0, buf1, 2 * near - 2, 1, mate).start()
 
     @pl.when(core == 1)
     def _():
-        for k in far[:-1]:
-            send(0, 2 * k + 1, gather[k] + 1, k).start()
+        for k in range(near - 1, 0, -1):
+            send(0, buf1, 2 * k - 1, 1, gather[k] + 1).start()
 
     sup[:, :TILE] = sup[:, :TILE] * jnp.where(
         sup[:, :TILE] >= thresh, W[0, 1].astype(F32), 0.0)
     sup[:, TILE:] = sup[:, TILE:] * jnp.where(
         sup[:, TILE:] >= thresh, A[0, 2].astype(F32), 0.0)
-
-    @pl.when(core == 1)
-    def _():
-        for k in range(len(gather)):
-            for c in (0, 1):
-                if k or not c:
-                    send(0, 2 * k + c, mate, k).wait_recv()
-        part = jnp.sum(rbuf[0, 0:2 * len(gather), :], axis=0, keepdims=True)
-        sbuf[1:2, :] = part
-        rbuf[1, 0:1, :] = part
-        count = len(spread)
-        for k in range(count - 1, -1, -1):
-            if k:
-                send(1, k, spread[k] + 1, k).start()
-            send(1, k, spread[k], count + k).start()
-        for k in range(1, count):
-            send(1, k, mate, k).wait_recv()
-
-    @pl.when(core == 0)
-    def _():
-        for k in range(len(spread)):
-            send(1, k, mate, k).wait_recv()
-
-    cnt_ref[...] = jnp.sum(rbuf[1, 0:len(spread), :], axis=0, keepdims=True)
-
     for c in moves:
         c.wait_send()
 
     @pl.when(core == 0)
     def _():
-        for k in far:
-            send(0, 2 * k, mate, k).wait_send()
+        send(0, buf1, 0, near, mate).wait_send()
+        send(2, buf3, 0, 1, mate).wait_recv()
 
     @pl.when(core == 1)
     def _():
-        for k in far[:-1]:
-            send(0, 2 * k + 1, mate, k).wait_send()
-        for k in range(2 * len(spread)):
-            if k:
-                send(1, 0, mate, k).wait_send()
+        send(0, buf1, 0, 2 * near - 1, mate).wait_recv()
+        part = jnp.sum(buf1[...], axis=0, keepdims=True)
+        sbuf[1:2, :] = part
+        buf2[wide - 1:wide, :] = part
+        for k in range(wide - 1, 0, -1):
+            send(1, buf2, k - 1, 1, spread[k] + 1).start()
+        send(0, buf1, 0, near - 1, mate).wait_send()
+        send(1, buf2, 0, wide - 1, mate).wait_recv()
+        whole = jnp.sum(buf2[...], axis=0, keepdims=True)
+        sbuf[2:3, :] = whole
+        send(2, buf3, 0, 1, mate).start()
+        buf3[0:1, :] = whole
+        send(1, buf2, 0, wide - 1, mate).wait_send()
+        send(2, buf3, 0, 1, mate).wait_send()
+
+    cnt_ref[...] = buf3[0, :3]
 
 
 def write_kernel(sup, cnt, out, counts, sem):
     copies = [
-        pltpu.make_async_copy(sup.at[pl.ds(128 * i, 128)], out.at[pl.ds(128 * i, 128)], sem.at[i])
-        for i in range(4)
-    ]
+        pltpu.make_async_copy(sup.at[pl.ds(64 * i, 64)], out.at[pl.ds(64 * i, 64)], sem.at[i])
+        for i in range(8)
+    ] + [pltpu.make_async_copy(cnt, counts, sem.at[8])]
     for c in copies:
         c.start()
-    counts[...] = cnt[0, :3]
     for c in copies:
         c.wait()
 
@@ -284,7 +284,6 @@
     vmem = pl.BlockSpec(memory_space=pltpu.VMEM)
     smem = pl.BlockSpec(memory_space=pltpu.SMEM)
     hbm = pl.BlockSpec(memory_space=pl.ANY)
-    slots = max(2 * group_size(GATHER), 2 * group_size(SPREAD))
     tiles = [
         pltpu.with_memory_space_constraint(x, pltpu.HBM)
         for x in (adj_diag, adj_right, alive_diag, alive_right)
@@ -293,7 +292,7 @@
         lambda *refs: peel_kernel(n, *refs),
         out_shape=(
             pltpu.VMEM((TILE, 2 * TILE), F32),
-            pltpu.VMEM((1, 128), I32),
+            pltpu.VMEM((3,), I32),
         ),
         in_specs=[pl.BlockSpec(memory_space=pltpu.HBM)] * 4 + [smem],
         out_specs=[vmem, vmem],
@@ -306,13 +305,15 @@
             pltpu.VMEM((TILE, TILE), F32),
             pltpu.VMEM((TILE, TILE), F32),
             pltpu.VMEM((TILE, TILE), F32),
-            pltpu.VMEM((2, 128), I32),
-            pltpu.VMEM((2, slots, 128), I32),
+            pltpu.VMEM((3, 128), I32),
+            pltpu.VMEM((2 * group_size(GATHER), 128), I32),
+            pltpu.VMEM((group_size(SPREAD), 128), I32),
+            pltpu.VMEM((1, 128), I32),
             pltpu.SemaphoreType.DMA((4,)),
             pltpu.SemaphoreType.DMA((6,)),
             pltpu.SemaphoreType.DMA((6,)),
-            pltpu.SemaphoreType.DMA((2, slots)),
-            pltpu.SemaphoreType.DMA((2, slots)),
+            pltpu.SemaphoreType.DMA((3,)),
+            pltpu.SemaphoreType.DMA((3,)),
         ],
         compiler_params=pltpu.CompilerParams(
             collective_id=0, has_side_effects=True, vmem_limit_bytes=40 * 2**20
@@ -326,8 +327,8 @@
             jax.ShapeDtypeStruct((3,), I32),
         ),
         in_specs=[vmem, vmem],
-        out_specs=[hbm, vmem],
-        scratch_shapes=[pltpu.SemaphoreType.DMA((4,))],
+        out_specs=[hbm, hbm],
+        scratch_shapes=[pltpu.SemaphoreType.DMA((9,))],
         compiler_params=pltpu.CompilerParams(vmem_limit_bytes=4 * 2**20),
         name="write",
     )(support, counts)

time: 39.4 us -> 36.4 us (0.924)
  Pallas kernels: 37.9 us -> 34.9 us
    pallas_call x1, Pallas kernels: 36 us -> 33.5 us  [on_device(): pl.pallas_call(lambda *refs: peel_kernel(n, *refs), out_shape=(pltpu.VMEM...]
    pallas_call x1, Pallas kernels: 1.86 us -> 1.39 us  [on_device(): pl.pallas_call(write_kernel, out_shape=(jax.ShapeDtypeStruct((TILE, 2 * T...]
where the time goes in v3:
time: 36.4 us; the launch traced here: 36.2 us
  Pallas kernels  34.9 us (96%)
  between operations  1.29 us (4%)
    pallas_call x1, Pallas kernels, on_device(): pl.pallas_call(lambda *refs: peel_kernel(n, *refs), out_shape=(pltpu.VMEM...  33.5 us
    pallas_call x1, Pallas kernels, on_device(): pl.pallas_call(write_kernel, out_shape=(jax.ShapeDtypeStruct((TILE, 2 * T...  1.39 us

profile of v3, /device:TPU:1, one launch (start us, length us, event | category | flops | bytes accessed | tf_op | source)
XLA Modules:
  0.0 36.2 jit_solution(9634687541965007270)
XLA Ops:
  1.3 33.5 %peel.1 = (f32[512,1024]{1,0:T(8,128)S(1)}, s32[3]{0:T(128)S(1)}) custom-call(s32[16,512]{1,0:T(8,128)} %refs_0_.1, s32[16,512]{1,0:T(8,128)} %refs_1_.1, s32[16,512]{1,0:T(8,128)} %refs_2_.1, s32[16,512]{1,0:T(8,128)} %refs_3_.1, s32[1]{0:T(128)S(6)} %copy.7.refs_4_), custom_call_target="tpu_custom_call" | custom-call | tf_op jit(solution)/shard_map/peel/pallas_call | solution.py:291
  34.8 1.4 %write.1 = (f32[512,1024]{1,0:T(8,128)}, s32[3]{0:T(128)}) custom-call(f32[512,1024]{1,0:T(8,128)S(1)} %get-tuple-element.4.sup, s32[3]{0:T(128)S(1)} %get-tuple-element.5.cnt), custom_call_target="tpu_custom_call" | custom-call | tf_op jit(solution)/shard_map/write/pallas_call | solution.py:323

commit v4 on v3

--- a/solution.py
+++ b/solution.py
@@ -16,6 +16,8 @@
 GATHER = (YAX,)
 SPREAD = (XAX, ZAX)
 
+PIECES = [(q, c) for q in range(4) for c in range(q, 4)]
+
 
 def chips_of(chip, axes):
     ids = [chip]
@@ -41,13 +43,13 @@
 
 
 def unpack(words):
-    bit = lax.broadcasted_iota(I32, (32, TILE), 0)
+    bit = lax.broadcasted_iota(I32, (32, words.shape[1]), 0)
     return (words >> bit) & 1
 
 
 def peel_kernel(
     n, ad, ar, ld, lr, th_ref, sup, cnt_ref,
-    raw, acr, wit, A, W, U, Pw, Qa, sbuf, buf1, buf2, buf3,
+    raw, acr, wit, A, W, Pw, Qa, sbuf, buf1, buf2, buf3,
     in_sem, x_send, x_recv, r_send, r_recv,
 ):
     me = lax.axis_index("rows")
@@ -56,6 +58,11 @@
     mate = chip + 1 - core
     gather = chips_of(chip, GATHER)
     spread = chips_of(chip, SPREAD)
+    place = lax.rem(lax.div(chip, XAX[0]), XAX[1])
+    plane_no = lax.div(chip, ZAX[0])
+    first = [chip - plane_no * ZAX[0] + (k - place) * XAX[0] for k in range(XAX[1])]
+    early_even = jnp.logical_and(core == 0, plane_no == 0)
+    late_even = jnp.logical_and(core == 0, plane_no > 0)
     dev = {k: lax.rem(me + k + n, n) for k in (-2, -1, 1, 2)}
 
     loads = [
@@ -73,15 +80,30 @@
     for k in dev:
         signal(dev[k])
 
+    near, wide = len(gather), len(spread)
+    deep = SPREAD[1][1]
+    line = sorted(range(1, near), key=lambda k: abs(k - near // 2))
     signal(mate)
-    for c in gather[1:]:
-        signal(c + 1)
+    for k in line:
+        signal(gather[k] + 1)
+
+        @pl.when(core == 1)
+        def _():
+            signal(gather[k])
 
     @pl.when(core == 1)
     def _():
-        for c in gather[1:]:
+        for k in sorted(
+            range(1, wide),
+            key=lambda k: abs(k % deep - deep // 2) + abs(k // deep - wide // deep // 2),
+        ):
+            signal(spread[k] + 1)
+        for c in first:
             signal(c)
-        for c in spread[1:]:
+
+    @pl.when(early_even)
+    def _():
+        for c in spread:
             signal(c + 1)
 
     loads[0].wait()
@@ -89,16 +111,23 @@
     acr[2] = raw[0] & raw[1]
     loads[2].wait()
     loads[3].wait()
-    wit[1] = raw[2] & raw[3]
-    even_count = 4 + len(gather)
-
-    @pl.when(core == 0)
+    for h, (q, c) in enumerate(PIECES):
+        row, lane = slice(4 * q, 4 * q + 4), slice(128 * c, 128 * c + 128)
+        at = slice(4 * (h % 2), 4 * (h % 2) + 4)
+        wit[1, h // 2, at, :] = raw[2, row, lane] & raw[3, row, lane]
+    even_count = 4 + near
+
+    @pl.when(late_even)
     def _():
         pl.semaphore_wait(barrier, even_count)
 
+    @pl.when(early_even)
+    def _():
+        pl.semaphore_wait(barrier, even_count + wide)
+
     @pl.when(core == 1)
     def _():
-        pl.semaphore_wait(barrier, even_count + len(gather) + len(spread) - 2)
+        pl.semaphore_wait(barrier, even_count + near - 1 + wide - 1 + len(first))
 
     plan = (
         (acr, 2, 1, 1), (wit, 1, -1, 2), (wit, 1, 1, 0), (acr, 2, -1, 3),
@@ -113,7 +142,8 @@
                 device_id=(dev[to],), device_id_type=MESH,
             )
         )
-        moves[-1].start()
+    for c in moves[:4]:
+        c.start()
 
     thresh = (th_ref[0] - 2).astype(F32)
 
@@ -122,12 +152,23 @@
             A[0, t, 32 * g:32 * g + 32, :] = unpack(acr[t, g:g + 1, :]).astype(F32).astype(F8)
 
     def open_within(t):
-        for g in range(WORDS):
-            r = lax.broadcasted_iota(I32, (32, TILE), 0) + 32 * g
-            c = lax.broadcasted_iota(I32, (32, TILE), 1)
-            U[32 * g:32 * g + 32, :] = jnp.where(c > r, unpack(wit[t, g:g + 1, :]), 0).astype(F32)
-        u = U[...]
-        W[0, t] = (u + u.T).astype(F8)
+        row = lax.broadcasted_iota(I32, (128, 128), 0)
+        col = lax.broadcasted_iota(I32, (128, 128), 1)
+        for h, (q, c) in enumerate(PIECES):
+            first = 4 * (h % 2)
+            block = jnp.concatenate(
+                [unpack(wit[t, h // 2, first + g:first + g + 1, :]) for g in range(4)], axis=0
+            )
+            if q == c:
+                block = jnp.where(col > row, block, 0)
+            block = block.astype(F32)
+            flip = block.T
+            up, across = pl.ds(128 * q, 128), pl.ds(128 * c, 128)
+            if q == c:
+                W[0, t, up, up] = (block + flip).astype(F8)
+            else:
+                W[0, t, up, across] = block.astype(F8)
+                W[0, t, across, up] = flip.astype(F8)
 
     def keep(x, old):
         return jnp.where(x >= thresh, old.astype(F32), 0.0)
@@ -152,41 +193,69 @@
     Pw[...] = dot(w, w) + dot_nt(a, a)
     Qa[...] = dot(w, a)
 
-    def from_left():
-        for i in (0, 2, 4):
-            moves[i].wait_recv()
+    for c in moves[4:]:
+        c.start()
+
+    def near_left():
+        moves[0].wait_recv()
+        moves[2].wait_recv()
         open_across(1)
         open_within(0)
-        open_across(0)
         W[1, 1] = keep(dot_tn(A[0, 1], A[0, 1]) + Pw[...], W[0, 1]).astype(F8)
         A[1, 1] = keep(between(0, 0), A[0, 1]).astype(F8)
+
+    def far_left():
+        moves[4].wait_recv()
+        open_across(0)
         W[1, 0] = keep(inside(0, 0), W[0, 0]).astype(F8)
 
-    def from_right():
-        for i in (1, 3, 5):
-            moves[i].wait_recv()
+    def near_right():
+        moves[1].wait_recv()
+        moves[3].wait_recv()
         open_within(2)
         open_across(3)
-        open_within(3)
         A[1, 2] = keep(dot(A[0, 2], W[0, 2]) + Qa[...], A[0, 2]).astype(F8)
         W[1, 2] = keep(inside(0, 2), W[0, 2]).astype(F8)
+
+    def far_right():
+        moves[5].wait_recv()
+        open_within(3)
         A[1, 3] = keep(between(0, 2), A[0, 3]).astype(F8)
 
-    last_chip = lax.rem(lax.div(chip, XAX[0]), XAX[1]) == XAX[1] - 1
-
-    @pl.when(last_chip)
-    def _():
-        from_left()
-        from_right()
-
-    @pl.when(jnp.logical_not(last_chip))
-    def _():
-        from_right()
-        from_left()
+    def second_left():
+        A[0, 1] = keep(between(1, 0), A[1, 1]).astype(F8)
+
+    def second_right():
+        W[0, 2] = keep(inside(1, 2), W[1, 2]).astype(F8)
+
+    @pl.when(place == XAX[1] - 1)
+    def _():
+        near_left()
+        far_left()
+        second_left()
+        near_right()
+        far_right()
+        second_right()
+
+    @pl.when(place == 0)
+    def _():
+        near_right()
+        far_right()
+        second_right()
+        near_left()
+        far_left()
+        second_left()
+
+    @pl.when(jnp.logical_and(place > 0, place < XAX[1] - 1))
+    def _():
+        near_right()
+        near_left()
+        far_right()
+        far_left()
+        second_right()
+        second_left()
 
     total.append(edges(W[1, 1].astype(F32), A[1, 2].astype(F32)))
-    A[0, 1] = keep(between(1, 0), A[1, 1]).astype(F8)
-    W[0, 2] = keep(inside(1, 2), W[1, 2]).astype(F8)
     w = keep(inside(1, 1), W[1, 1])
     W[0, 1] = w.astype(F8)
     a = keep(between(1, 1), A[1, 2])
@@ -206,7 +275,7 @@
     for i in range(3):
         lost = (total[i] - total[i + 1]).astype(I32)
         acc = jnp.where(lane == i, lost, acc)
-    near, wide = len(gather), len(spread)
+    plane = sorted(range(1, wide), key=lambda k: (k % deep - 2) % deep)
     sbuf[0:1, :] = acc
     buf1[2 * near - 1:2 * near, :] = acc
 
@@ -220,13 +289,13 @@
 
     @pl.when(core == 0)
     def _():
-        for k in range(near - 1, 0, -1):
+        for k in line:
             send(0, buf1, 2 * k - 2, 1, gather[k] + 1).start()
         send(0, buf1, 2 * near - 2, 1, mate).start()
 
     @pl.when(core == 1)
     def _():
-        for k in range(near - 1, 0, -1):
+        for k in line:
             send(0, buf1, 2 * k - 1, 1, gather[k] + 1).start()
 
     sup[:, :TILE] = sup[:, :TILE] * jnp.where(
@@ -239,7 +308,16 @@
     @pl.when(core == 0)
     def _():
         send(0, buf1, 0, near, mate).wait_send()
+
+    @pl.when(late_even)
+    def _():
         send(2, buf3, 0, 1, mate).wait_recv()
+        cnt_ref[...] = buf3[0, :3]
+
+    @pl.when(early_even)
+    def _():
+        send(1, buf2, 0, wide, mate).wait_recv()
+        cnt_ref[...] = jnp.sum(buf2[...], axis=0)[:3]
 
     @pl.when(core == 1)
     def _():
@@ -247,18 +325,23 @@
         part = jnp.sum(buf1[...], axis=0, keepdims=True)
         sbuf[1:2, :] = part
         buf2[wide - 1:wide, :] = part
-        for k in range(wide - 1, 0, -1):
+        for k in plane:
             send(1, buf2, k - 1, 1, spread[k] + 1).start()
+        for c in first:
+            send(1, buf2, plane_no * XAX[1] + place, 1, c).start()
         send(0, buf1, 0, near - 1, mate).wait_send()
         send(1, buf2, 0, wide - 1, mate).wait_recv()
         whole = jnp.sum(buf2[...], axis=0, keepdims=True)
-        sbuf[2:3, :] = whole
-        send(2, buf3, 0, 1, mate).start()
-        buf3[0:1, :] = whole
+        cnt_ref[...] = whole[0, :3]
+
+        @pl.when(plane_no > 0)
+        def _():
+            sbuf[2:3, :] = whole
+            send(2, buf3, 0, 1, mate).start()
+            send(2, buf3, 0, 1, mate).wait_send()
+
         send(1, buf2, 0, wide - 1, mate).wait_send()
-        send(2, buf3, 0, 1, mate).wait_send()
-
-    cnt_ref[...] = buf3[0, :3]
+        send(1, buf2, 0, len(first), mate).wait_send()
 
 
 def write_kernel(sup, cnt, out, counts, sem):
@@ -299,10 +382,9 @@
         scratch_shapes=[
             pltpu.VMEM((4, WORDS, TILE), I32),
             pltpu.VMEM((HALF, WORDS, TILE), I32),
-            pltpu.VMEM((HALF, WORDS, TILE), I32),
+            pltpu.VMEM((HALF, len(PIECES) // 2, 8, 128), I32),
             pltpu.VMEM((2, HALF, TILE, TILE), F8),
             pltpu.VMEM((2, HALF, TILE, TILE), F8),
-            pltpu.VMEM((TILE, TILE), F32),
             pltpu.VMEM((TILE, TILE), F32),
             pltpu.VMEM((TILE, TILE), F32),
             pltpu.VMEM((3, 128), I32),

time: 36.4 us -> 35.2 us (0.967)
  Pallas kernels: 34.9 us -> 33.7 us
    pallas_call x1, Pallas kernels: 33.5 us -> 32.3 us  [on_device(): pl.pallas_call(lambda *refs: peel_kernel(n, *refs), out_shape=(pltpu.VMEM...]
where the time goes in v4:
time: 35.2 us; the launch traced here: 35 us
  Pallas kernels  33.7 us (96%)
  between operations  1.29 us (4%)
    pallas_call x1, Pallas kernels, on_device(): pl.pallas_call(lambda *refs: peel_kernel(n, *refs), out_shape=(pltpu.VMEM...  32.3 us
    pallas_call x1, Pallas kernels, on_device(): pl.pallas_call(write_kernel, out_shape=(jax.ShapeDtypeStruct((TILE, 2 * T...  1.39 us

profile of v4, /device:TPU:1, one launch (start us, length us, event | category | flops | bytes accessed | tf_op | source)
XLA Modules:
  0.0 35.0 jit_solution(13655997977480097067)
XLA Ops:
  1.3 32.3 %peel.1 = (f32[512,1024]{1,0:T(8,128)S(1)}, s32[3]{0:T(128)S(1)}) custom-call(s32[16,512]{1,0:T(8,128)} %refs_0_.1, s32[16,512]{1,0:T(8,128)} %refs_1_.1, s32[16,512]{1,0:T(8,128)} %refs_2_.1, s32[16,512]{1,0:T(8,128)} %refs_3_.1, s32[1]{0:T(128)S(6)} %copy.7.refs_4_), custom_call_target="tpu_custom_call" | custom-call | tf_op jit(solution)/shard_map/peel/pallas_call | solution.py:374
  33.6 1.4 %write.1 = (f32[512,1024]{1,0:T(8,128)}, s32[3]{0:T(128)}) custom-call(f32[512,1024]{1,0:T(8,128)S(1)} %get-tuple-element.4.sup, s32[3]{0:T(128)S(1)} %get-tuple-element.5.cnt), custom_call_target="tpu_custom_call" | custom-call | tf_op jit(solution)/shard_map/write/pallas_call | solution.py:405

commit v5 on v4

--- a/solution.py
+++ b/solution.py
@@ -13,8 +13,8 @@
 I32 = jnp.int32
 MESH = pl.DeviceIdType.MESH
 XAX, YAX, ZAX = (2, 4), (8, 8), (64, 8)
-GATHER = (YAX,)
-SPREAD = (XAX, ZAX)
+GATHER = (XAX,)
+SPREAD = (YAX, ZAX)
 
 PIECES = [(q, c) for q in range(4) for c in range(q, 4)]
 
@@ -60,7 +60,9 @@
     spread = chips_of(chip, SPREAD)
     place = lax.rem(lax.div(chip, XAX[0]), XAX[1])
     plane_no = lax.div(chip, ZAX[0])
-    first = [chip - plane_no * ZAX[0] + (k - place) * XAX[0] for k in range(XAX[1])]
+    outer, length = SPREAD[0]
+    spot = lax.rem(lax.div(chip, outer), length)
+    first = [chip - plane_no * ZAX[0] + (k - spot) * outer for k in range(length)]
     early_even = jnp.logical_and(core == 0, plane_no == 0)
     late_even = jnp.logical_and(core == 0, plane_no > 0)
     dev = {k: lax.rem(me + k + n, n) for k in (-2, -1, 1, 2)}
@@ -83,28 +85,27 @@
     near, wide = len(gather), len(spread)
     deep = SPREAD[1][1]
     line = sorted(range(1, near), key=lambda k: abs(k - near // 2))
-    signal(mate)
-    for k in line:
-        signal(gather[k] + 1)
-
-        @pl.when(core == 1)
-        def _():
+
+    @pl.when(core == 1)
+    def _():
+        for k in line:
+            signal(gather[k] + 1)
             signal(gather[k])
-
-    @pl.when(core == 1)
-    def _():
         for k in sorted(
             range(1, wide),
             key=lambda k: abs(k % deep - deep // 2) + abs(k // deep - wide // deep // 2),
         ):
             signal(spread[k] + 1)
-        for c in first:
-            signal(c)
+        signal(mate)
 
     @pl.when(early_even)
     def _():
         for c in spread:
             signal(c + 1)
+
+    @pl.when(late_even)
+    def _():
+        signal(mate)
 
     loads[0].wait()
     loads[1].wait()
@@ -115,19 +116,17 @@
         row, lane = slice(4 * q, 4 * q + 4), slice(128 * c, 128 * c + 128)
         at = slice(4 * (h % 2), 4 * (h % 2) + 4)
         wit[1, h // 2, at, :] = raw[2, row, lane] & raw[3, row, lane]
-    even_count = 4 + near
-
-    @pl.when(late_even)
-    def _():
-        pl.semaphore_wait(barrier, even_count)
-
-    @pl.when(early_even)
-    def _():
-        pl.semaphore_wait(barrier, even_count + wide)
-
-    @pl.when(core == 1)
-    def _():
-        pl.semaphore_wait(barrier, even_count + near - 1 + wide - 1 + len(first))
+    @pl.when(core == 0)
+    def _():
+        pl.semaphore_wait(barrier, 4 + near)
+
+    @pl.when(jnp.logical_and(core == 1, plane_no > 0))
+    def _():
+        pl.semaphore_wait(barrier, 4 + near - 1 + wide - 1 + len(first) + 1)
+
+    @pl.when(jnp.logical_and(core == 1, plane_no == 0))
+    def _():
+        pl.semaphore_wait(barrier, 4 + near - 1 + wide - 1 + len(first))
 
     plan = (
         (acr, 2, 1, 1), (wit, 1, -1, 2), (wit, 1, 1, 0), (acr, 2, -1, 3),
@@ -275,7 +274,7 @@
     for i in range(3):
         lost = (total[i] - total[i + 1]).astype(I32)
         acc = jnp.where(lane == i, lost, acc)
-    plane = sorted(range(1, wide), key=lambda k: (k % deep - 2) % deep)
+    plane = sorted(range(1, wide), key=lambda k: ((k % deep - 1) % deep, abs(k // deep - length // 2)))
     sbuf[0:1, :] = acc
     buf1[2 * near - 1:2 * near, :] = acc
 
@@ -328,7 +327,7 @@
         for k in plane:
             send(1, buf2, k - 1, 1, spread[k] + 1).start()
         for c in first:
-            send(1, buf2, plane_no * XAX[1] + place, 1, c).start()
+            send(1, buf2, plane_no * length + spot, 1, c).start()
         send(0, buf1, 0, near - 1, mate).wait_send()
         send(1, buf2, 0, wide - 1, mate).wait_recv()
         whole = jnp.sum(buf2[...], axis=0, keepdims=True)

time: 35.2 us -> 34.8 us (0.989)
  no operation moved by 1% of the time
where the time goes in v5:
time: 34.8 us; the launch traced here: 34.6 us
  Pallas kernels  33.4 us (96%)
  between operations  1.29 us (4%)
    pallas_call x1, Pallas kernels, on_device(): pl.pallas_call(lambda *refs: peel_kernel(n, *refs), out_shape=(pltpu.VMEM...  32 us
    pallas_call x1, Pallas kernels, on_device(): pl.pallas_call(write_kernel, out_shape=(jax.ShapeDtypeStruct((TILE, 2 * T...  1.39 us

profile of v5, /device:TPU:1, one launch (start us, length us, event | category | flops | bytes accessed | tf_op | source)
XLA Modules:
  0.0 34.6 jit_solution(2172618092466036342)
XLA Ops:
  1.3 32.0 %peel.1 = (f32[512,1024]{1,0:T(8,128)S(1)}, s32[3]{0:T(128)S(1)}) custom-call(s32[16,512]{1,0:T(8,128)} %refs_0_.1, s32[16,512]{1,0:T(8,128)} %refs_1_.1, s32[16,512]{1,0:T(8,128)} %refs_2_.1, s32[16,512]{1,0:T(8,128)} %refs_3_.1, s32[1]{0:T(128)S(6)} %copy.7.refs_4_), custom_call_target="tpu_custom_call" | custom-call | tf_op jit(solution)/shard_map/peel/pallas_call | solution.py:373
  33.3 1.4 %write.1 = (f32[512,1024]{1,0:T(8,128)}, s32[3]{0:T(128)}) custom-call(f32[512,1024]{1,0:T(8,128)S(1)} %get-tuple-element.4.sup, s32[3]{0:T(128)S(1)} %get-tuple-element.5.cnt), custom_call_target="tpu_custom_call" | custom-call | tf_op jit(solution)/shard_map/write/pallas_call | solution.py:404

commit v6 on v5

--- a/solution.py
+++ b/solution.py
@@ -116,34 +116,6 @@
         row, lane = slice(4 * q, 4 * q + 4), slice(128 * c, 128 * c + 128)
         at = slice(4 * (h % 2), 4 * (h % 2) + 4)
         wit[1, h // 2, at, :] = raw[2, row, lane] & raw[3, row, lane]
-    @pl.when(core == 0)
-    def _():
-        pl.semaphore_wait(barrier, 4 + near)
-
-    @pl.when(jnp.logical_and(core == 1, plane_no > 0))
-    def _():
-        pl.semaphore_wait(barrier, 4 + near - 1 + wide - 1 + len(first) + 1)
-
-    @pl.when(jnp.logical_and(core == 1, plane_no == 0))
-    def _():
-        pl.semaphore_wait(barrier, 4 + near - 1 + wide - 1 + len(first))
-
-    plan = (
-        (acr, 2, 1, 1), (wit, 1, -1, 2), (wit, 1, 1, 0), (acr, 2, -1, 3),
-        (acr, 2, 2, 0), (wit, 1, -2, 3),
-    )
-    moves = []
-    for i, (ref, src, to, dst) in enumerate(plan):
-        moves.append(
-            pltpu.make_async_remote_copy(
-                src_ref=ref.at[src], dst_ref=ref.at[dst],
-                send_sem=x_send.at[i], recv_sem=x_recv.at[i],
-                device_id=(dev[to],), device_id_type=MESH,
-            )
-        )
-    for c in moves[:4]:
-        c.start()
-
     thresh = (th_ref[0] - 2).astype(F32)
 
     def open_across(t):
@@ -191,6 +163,34 @@
     total = [edges(w.astype(F32), a.astype(F32))]
     Pw[...] = dot(w, w) + dot_nt(a, a)
     Qa[...] = dot(w, a)
+
+    @pl.when(core == 0)
+    def _():
+        pl.semaphore_wait(barrier, 4 + near)
+
+    @pl.when(jnp.logical_and(core == 1, plane_no > 0))
+    def _():
+        pl.semaphore_wait(barrier, 4 + near - 1 + wide - 1 + len(first) + 1)
+
+    @pl.when(jnp.logical_and(core == 1, plane_no == 0))
+    def _():
+        pl.semaphore_wait(barrier, 4 + near - 1 + wide - 1 + len(first))
+
+    plan = (
+        (acr, 2, 1, 1), (wit, 1, -1, 2), (wit, 1, 1, 0), (acr, 2, -1, 3),
+        (acr, 2, 2, 0), (wit, 1, -2, 3),
+    )
+    moves = []
+    for i, (ref, src, to, dst) in enumerate(plan):
+        moves.append(
+            pltpu.make_async_remote_copy(
+                src_ref=ref.at[src], dst_ref=ref.at[dst],
+                send_sem=x_send.at[i], recv_sem=x_recv.at[i],
+                device_id=(dev[to],), device_id_type=MESH,
+            )
+        )
+    for c in moves[:4]:
+        c.start()
 
     for c in moves[4:]:
         c.start()

time: 34.8 us -> 34.8 us (level)
  no operation moved by 1% of the time
where the time goes in v6:
time: 34.8 us; the launch traced here: 34.6 us
  Pallas kernels  33.4 us (96%)
  between operations  1.29 us (4%)
    pallas_call x1, Pallas kernels, on_device(): pl.pallas_call(lambda *refs: peel_kernel(n, *refs), out_shape=(pltpu.VMEM...  32 us
    pallas_call x1, Pallas kernels, on_device(): pl.pallas_call(write_kernel, out_shape=(jax.ShapeDtypeStruct((TILE, 2 * T...  1.39 us

profile of v6, /device:TPU:1, one launch (start us, length us, event | category | flops | bytes accessed | tf_op | source)
XLA Modules:
  0.0 34.6 jit_solution(3849734918860485807)
XLA Ops:
  1.3 32.0 %peel.1 = (f32[512,1024]{1,0:T(8,128)S(1)}, s32[3]{0:T(128)S(1)}) custom-call(s32[16,512]{1,0:T(8,128)} %refs_0_.1, s32[16,512]{1,0:T(8,128)} %refs_1_.1, s32[16,512]{1,0:T(8,128)} %refs_2_.1, s32[16,512]{1,0:T(8,128)} %refs_3_.1, s32[1]{0:T(128)S(6)} %copy.7.refs_4_), custom_call_target="tpu_custom_call" | custom-call | tf_op jit(solution)/shard_map/peel/pallas_call | solution.py:373
  33.3 1.4 %write.1 = (f32[512,1024]{1,0:T(8,128)}, s32[3]{0:T(128)}) custom-call(f32[512,1024]{1,0:T(8,128)S(1)} %get-tuple-element.4.sup, s32[3]{0:T(128)S(1)} %get-tuple-element.5.cnt), custom_call_target="tpu_custom_call" | custom-call | tf_op jit(solution)/shard_map/write/pallas_call | solution.py:404
